TPU v7x, 256 devices: a whole 4x4x8 slice. The times are simulated.
256 devices in a mesh: a3: 8 (over z), a2: 4 (over y), a1: 8 (over x, core).
Axes of the slice: x: 4, y: 4, z: 8, core: 2. Of those that a mesh axis runs over, the one named last changes fastest.
Arguments:
- tensor: bfloat16 [384, 1024, 1024], P('a1', 'a2', 'a3')
- u_time: float32 [384, 48], replicated
- u_height: float32 [1024, 128], replicated
- u_width: float32 [1024, 128], replicated
Outputs:
- output 1: float32 [384, 48], replicated
- output 2: float32 [1024, 128], replicated
- output 3: float32 [1024, 128], replicated
- output 4: float32 [48, 128, 128], P('a1', 'a2', 'a3')
- output 5: float32 [], replicated
All inputs are finite; a program needn't handle non-finite values.
Results may differ from a plain program's by a relative error of at most 0.00243.
Values are sent between devices in bfloat16 or wider.
A program may use at most 768 MiB of HBM per device.

v0:
```python
import jax
import jax.numpy as jnp
from jax import lax
from jax.sharding import PartitionSpec as P


def rows_of(factor, axis_name, count):
    start_row = lax.axis_index(axis_name) * count
    return lax.dynamic_slice_in_dim(factor, start_row, count, 0).astype(jnp.bfloat16)


def gram_update(local_rows, row_axes, sum_axes, factor):
    all_rows = lax.all_gather(local_rows, row_axes, axis=0, tiled=True)
    gram_part = lax.dot_general(local_rows, all_rows, (((1,), (1,)), ((), ())), preferred_element_type=jnp.float32)
    gram_rows = lax.psum(gram_part, sum_axes).astype(jnp.bfloat16)
    power_cols = jnp.dot(gram_rows, factor.astype(jnp.bfloat16), preferred_element_type=jnp.float32)
    col_sq = lax.psum(jnp.sum(power_cols * power_cols, axis=0, keepdims=True), row_axes)
    return lax.all_gather(power_cols / jnp.sqrt(col_sq), row_axes, axis=0, tiled=True)


def solution(mesh):
    def local_sweep(tensor, u_time, u_height, u_width):
        frames, grid_h, grid_w = tensor.shape
        t_part = jnp.dot(tensor.reshape(frames * grid_h, grid_w), rows_of(u_width, 'a3', grid_w), preferred_element_type=jnp.float32)
        t_mat = lax.psum_scatter(t_part.reshape(frames, grid_h, -1), 'a3', scatter_dimension=2, tiled=True).astype(jnp.bfloat16)
        y1_part = jnp.einsum('ihc,hb->icb', t_mat, rows_of(u_height, 'a2', grid_h), preferred_element_type=jnp.float32)
        y_one = lax.psum_scatter(y1_part, 'a2', scatter_dimension=2, tiled=True).astype(jnp.bfloat16)
        new_time = gram_update(y_one.reshape(frames, -1), 'a1', ('a2', 'a3'), u_time)
        time_rows = rows_of(new_time, 'a1', frames)
        y2_part = jnp.einsum('ihc,ia->hca', t_mat, time_rows, preferred_element_type=jnp.float32)
        y_two = lax.psum_scatter(y2_part, 'a1', scatter_dimension=2, tiled=True).astype(jnp.bfloat16)
        new_height = gram_update(y_two.reshape(grid_h, -1), 'a2', ('a1', 'a3'), u_height)
        z_part = lax.dot_general(time_rows, tensor.reshape(frames, grid_h * grid_w), (((0,), (0,)), ((), ())), preferred_element_type=jnp.float32)
        z_mat = lax.psum_scatter(z_part, 'a1', scatter_dimension=0, tiled=True).astype(jnp.bfloat16).reshape(-1, grid_h, grid_w)
        y3_part = jnp.einsum('ahw,hb->wab', z_mat, rows_of(new_height, 'a2', grid_h), preferred_element_type=jnp.float32)
        y_three = lax.psum_scatter(y3_part, 'a2', scatter_dimension=2, tiled=True).astype(jnp.bfloat16)
        new_width = gram_update(y_three.reshape(grid_w, -1), 'a3', ('a1', 'a2'), u_width)
        core_part = jnp.einsum('wab,wc->abc', y_three, rows_of(new_width, 'a3', grid_w), preferred_element_type=jnp.float32)
        core_tensor = lax.psum_scatter(core_part, 'a3', scatter_dimension=2, tiled=True)
        core_energy = lax.psum(jnp.sum(core_tensor * core_tensor), ('a1', 'a2', 'a3'))
        return new_time, new_height, new_width, core_tensor, core_energy

    return jax.shard_map(local_sweep, mesh=mesh, in_specs=(P('a1', 'a2', 'a3'), P(), P(), P()), out_specs=(P(), P(), P(), P('a1', 'a2', 'a3'), P()), check_vma=False)
```

profile of v0, /device:TPU:1, one launch (start us, length us, event | category | flops | bytes accessed | tf_op | source)
XLA Modules:
  0.0 1010.4 jit_solution(8321157034219148761)
XLA Ops:
  10.2 4.6 copy.37
  14.9 78.8 %reduce-scatter.8.cloned.1.call-done = f32[48,256,16]{1,0,2:T(8,128)} async-done(((f32[48,256,128]{1,0,2:T(8,128)}), f32[48,256,16]{1,0,2:T(8,128)}) %reduce-scatter.8.cloned.1.call-update) | async-done | bytes 786448 | tf_op jit(solution)/shard_map/reduce_scatter | solution.py:25
  96.5 23.5 %reduce-scatter.10.cloned.1.call-done = f32[48,16,32]{0,1,2:T(8,128)} async-done(((f32[48,16,128]{0,1,2:T(8,128)}), f32[48,16,32]{0,1,2:T(8,128)}) %reduce-scatter.10.cloned.1.call-update) | async-done | bytes 98320 | tf_op jit(solution)/shard_map/reduce_scatter | solution.py:27
  121.4 15.6 %all_gather.18 = bf16[384,512]{1,0:T(8,128)(2,1)S(1)} all-gather(bf16[48,512]{1,0:T(8,128)(2,1)S(1)} %reshape.33), channel_id=1, replica_groups=mesh['a3'=8,'a2'=4,'a1'=8] {'a1'}, dimensions={0}, use_global_device_ids=true | all-gather | bytes 442368 | tf_op jit(solution)/shard_map/all_gather | solution.py:13
  137.2 113.3 %psum.49 = bf16[48,384]{1,0:T(8,128)(2,1)S(1)} all-reduce(f32[48,384]{1,0:T(8,128)S(1)} %fusion.35), channel_id=1, replica_groups=mesh['a3'=8,'a2'=4,'a1'=8] {'a2','a3'}, use_global_device_ids=true, to_apply=%region_2.0 | all-reduce | flops 18432 | bytes 110592 | tf_op jit(solution)/shard_map/psum | solution.py:15
  250.6 39.4 %psum.50 = f32[1,48]{1,0:T(1,128)S(1)} all-reduce(f32[1,48]{1,0:T(1,128)S(1)} %bitcast.61), channel_id=1, replica_groups=mesh['a3'=8,'a2'=4,'a1'=8] {'a1'}, use_global_device_ids=true, to_apply=%region_4.0 | all-reduce | flops 48 | bytes 384 | tf_op jit(solution)/shard_map/psum | solution.py:17
  290.1 13.3 %all_gather.19 = f32[384,48]{1,0:T(8,128)S(1)} all-gather(f32[48,48]{1,0:T(8,128)S(1)} %broadcast_divide_fusion.2), channel_id=1, replica_groups=mesh['a3'=8,'a2'=4,'a1'=8] {'a1'}, dimensions={0}, use_global_device_ids=true | all-gather | bytes 82944 | tf_op jit(solution)/shard_map/all_gather | solution.py:18
  303.4 5.3 fusion.1
  310.4 53.0 %fusion = f32[8,32768]{1,0:T(8,128)S(1)} fusion(f32[48,32768]{1,0:T(8,128)} %fusion.1), kind=kCustom, calls=%all-reduce-scatter | all-reduce-scatter fusion | flops 2097153 | bytes 7341056
  363.4 4.4 collective-permute-start
  367.9 3.0 collective-permute-start.1
  372.2 13.0 %collective-permute-done.1 = bf16[6,32768]{1,0:T(8,128)(2,1)} collective-permute-done((bf16[6,32768]{1,0:T(8,128)(2,1)S(1)}, bf16[6,32768]{1,0:T(8,128)(2,1)}, u32[]{:S(2)}, u32[]{:S(2)}) %collective-permute-start.1) | collective-permute-done | bytes 393248
  385.2 4.5 concatenate
  391.0 9.2 all_gather.20
  400.5 246.8 %all-reduce.4 = bf16[256,1024]{1,0:T(8,128)(2,1)S(1)} all-reduce(f32[256,1024]{1,0:T(8,128)S(1)} %fusion.36), channel_id=1, replica_groups=mesh['a3'=8,'a2'=4,'a1'=8] {'a1','a3'}, use_global_device_ids=true, to_apply=%region_6.0 | all-reduce | flops 262144 | bytes 1572864 | tf_op jit(solution)/shard_map/psum | solution.py:15
  647.6 8.3 psum.52
  655.9 10.2 %all_gather.21 = f32[1024,128]{1,0:T(8,128)S(1)} all-gather(f32[256,128]{1,0:T(8,128)S(1)} %broadcast_divide_fusion), channel_id=1, replica_groups=mesh['a3'=8,'a2'=4,'a1'=8] {'a2'}, dimensions={0}, use_global_device_ids=true | all-gather | bytes 655360 | tf_op jit(solution)/shard_map/all_gather | solution.py:18
  667.2 26.5 %reduce-scatter.14.cloned.1.call-done = f32[128,6,32]{0,2,1:T(8,128)} async-done(((f32[128,6,128]{0,2,1:T(8,128)}), f32[128,6,32]{0,2,1:T(8,128)}) %reduce-scatter.14.cloned.1.call-update) | async-done | bytes 98320 | tf_op jit(solution)/shard_map/reduce_scatter | solution.py:36
  694.6 21.6 %all_gather.22 = bf16[1024,192]{0,1:T(8,128)(2,1)S(1)} all-gather(bf16[128,192]{0,1:T(8,128)(2,1)S(1)} %bitcast.59), channel_id=1, replica_groups=mesh['a3'=8,'a2'=4,'a1'=8] {'a3'}, dimensions={0}, use_global_device_ids=true | all-gather | bytes 442368 | tf_op jit(solution)/shard_map/all_gather | solution.py:13
  716.4 131.9 %all-reduce.5 = bf16[128,1024]{1,0:T(8,128)(2,1)S(1)} all-reduce(f32[128,1024]{1,0:T(8,128)S(1)} %fusion.37), channel_id=1, replica_groups=mesh['a3'=8,'a2'=4,'a1'=8] {'a1','a2'}, use_global_device_ids=true, to_apply=%region_11.0 | all-reduce | flops 131072 | bytes 786432 | tf_op jit(solution)/shard_map/psum | solution.py:15
  848.6 11.9 %psum.54 = f32[1,128]{1,0:T(1,128)S(1)} all-reduce(f32[1,128]{1,0:T(1,128)S(1)} %bitcast.63), channel_id=1, replica_groups=mesh['a3'=8,'a2'=4,'a1'=8] {'a3'}, use_global_device_ids=true, to_apply=%region_13.0 | all-reduce | flops 128 | bytes 1024 | tf_op jit(solution)/shard_map/psum | solution.py:17
  860.6 19.6 %all_gather.23 = f32[1024,128]{1,0:T(8,128)S(1)} all-gather(f32[128,128]{1,0:T(8,128)S(1)} %broadcast_divide_fusion.1), channel_id=1, replica_groups=mesh['a3'=8,'a2'=4,'a1'=8] {'a3'}, dimensions={0}, use_global_device_ids=true | all-gather | bytes 589824 | tf_op jit(solution)/shard_map/all_gather | solution.py:18
  881.9 39.1 %reduce-scatter.16.cloned.1.call-done = f32[6,32,16]{1,2,0:T(8,128)} async-done(((f32[6,32,128]{1,2,0:T(8,128)}), f32[6,32,16]{1,2,0:T(8,128)}) %reduce-scatter.16.cloned.1.call-update) | async-done | bytes 12304 | tf_op jit(solution)/shard_map/reduce_scatter | solution.py:39
  922.5 79.8 %psum.55 = f32[]{:T(128)} all-reduce(f32[]{:T(128)} %multiply_reduce_fusion.2), channel_id=1, replica_groups=mesh['a3'=8,'a2'=4,'a1'=8] {'a1','a2','a3'}, use_global_device_ids=true, to_apply=%region_16.0 | all-reduce | flops 1 | bytes 8 | tf_op jit(solution)/shard_map/psum | solution.py:40
  (58 shorter events, 19.2 us)
Async XLA Ops:
  7.2 86.5 %reduce-scatter.8.cloned.1.call-start = ((), (), s32[]{:S(2)}) async-start(), calls=%async_computation.5 | async-start | bytes 7077888 | tf_op jit(solution)/shard_map/reduce_scatter | solution.py:25
  14.8 288.6 %copy-start = (bf16[48,256,128]{2,1,0:T(8,128)(2,1)S(1)}, bf16[48,256,128]{2,1,0:T(8,128)(2,1)}, u32[]{:S(2)}) copy-start(bf16[48,256,128]{2,1,0:T(8,128)(2,1)} %param.4) | copy-start | bytes 9437188
  14.8 105.2 %reduce-scatter.10.cloned.1.call-start = ((), (), s32[]{:S(2)}) async-start(), calls=%async_computation.6 | async-start | bytes 1310720 | tf_op jit(solution)/shard_map/reduce_scatter | solution.py:27
  96.4 154.1 %copy-start.4 = (f32[384,48]{0,1:T(8,128)S(1)}, f32[384,48]{0,1:T(8,128)}, u32[]{:S(2)}) copy-start(f32[384,48]{0,1:T(8,128)} %param.5) | copy-start | bytes 221188
  96.5 293.5 %reduce-scatter.12.cloned.1.call-start = ((), (), s32[]{:S(2)}) async-start(), calls=%async_computation.7 | async-start | bytes 884736 | tf_op jit(solution)/shard_map/reduce_scatter | solution.py:31
  303.4 5.3 copy-start.1
  310.3 60.6 %copy-start.5 = (u32[256]{0:T(256)S(1)}, u32[256]{0:T(256)}, u32[]{:S(2)}) copy-start(u32[256]{0:T(256)} %constant.28) | copy-start | bytes 3076
  310.3 383.4 %reduce-scatter.14.cloned.1.call-start = ((), (), s32[]{:S(2)}) async-start(), calls=%async_computation.8 | async-start | bytes 491520 | tf_op jit(solution)/shard_map/reduce_scatter | solution.py:36
  363.4 21.7 %collective-permute-start = (bf16[8,32768]{1,0:T(8,128)(2,1)S(1)}, bf16[8,32768]{1,0:T(8,128)(2,1)S(1)}, u32[]{:S(2)}, u32[]{:S(2)}) collective-permute-start(bf16[8,32768]{1,0:T(8,128)(2,1)S(1)} %convert), channel_id=1, source_target_pairs={{0,1},{1,2},{2,3},{3,4},{4,5},{5,6},{6,7},{8,9},{9,10},{10,11},{11... | collective-permute-start | bytes 1572872
  367.9 17.2 %collective-permute-start.1 = (bf16[6,32768]{1,0:T(8,128)(2,1)S(1)}, bf16[6,32768]{1,0:T(8,128)(2,1)}, u32[]{:S(2)}, u32[]{:S(2)}) collective-permute-start(bf16[6,32768]{1,0:T(8,128)(2,1)S(1)} %slice), channel_id=1, source_target_pairs={{0,2},{1,3},{2,4},{3,5},{4,6},{5,7},{8,10},{9,11},{10,12},{11,13},... | collective-permute-start | bytes 1179656
  389.9 257.4 %copy-start.2 = (f32[1024,128]{1,0:T(8,128)S(1)}, f32[1024,128]{1,0:T(8,128)}, u32[]{:S(2)}) copy-start(f32[1024,128]{1,0:T(8,128)} %param.6) | copy-start | bytes 1572868
  647.3 201.1 %copy-start.3 = (f32[1024,128]{1,0:T(8,128)S(1)}, f32[1024,128]{1,0:T(8,128)}, u32[]{:S(2)}) copy-start(f32[1024,128]{1,0:T(8,128)} %param.7) | copy-start | bytes 1572868
  667.1 253.9 %reduce-scatter.16.cloned.1.call-start = ((), (), s32[]{:S(2)}) async-start(), calls=%async_computation.9 | async-start | bytes 442368 | tf_op jit(solution)/shard_map/reduce_scatter | solution.py:39
Sparse Core Ops, SparseCore 0:
  14.9 78.6 reduce-scatter.7
  96.6 23.4 reduce-scatter.9
  310.4 24.3 reduce-scatter.11
  667.2 26.4 reduce-scatter.13
  881.3 39.7 reduce-scatter.15
where the time goes:
time: 1010 us
  blocking collectives  774 us (77%)
  waiting for transfers between devices  181 us (18%)
  local copies, waits for them, and re-layouts  15.6 us (2%)
  between operations  14.6 us (1%)
  matrix products  13.4 us (1%)
    psum x3, blocking collectives, gram_update(): gram_rows = lax.psum(gram_part, sum_axes).astype(jnp.bfloat16)  492 us
    psum x1, blocking collectives, local_sweep(): lax.psum(jnp.sum(core_tensor * core_tensor), ('a1', 'a2', 'a3'))  79.8 us
    reduce_scatter x1, waiting for transfers between devices, local_sweep(): lax.psum_scatter(t_part.reshape(frames, grid_h, -1), 'a3', scatter_dimens...  78.8 us
    psum x3, blocking collectives, gram_update(): lax.psum(jnp.sum(power_cols * power_cols, axis=0, keepdims=True), row_axes)  59.6 us
    unnamed x1, blocking collectives  53 us
    all_gather x3, blocking collectives, gram_update(): all_rows = lax.all_gather(local_rows, row_axes, axis=0, tiled=True)  46.4 us
    all_gather x3, blocking collectives, gram_update(): lax.all_gather(power_cols / jnp.sqrt(col_sq), row_axes, axis=0, tiled=True)  43 us
    reduce_scatter x1, waiting for transfers between devices, local_sweep(): lax.psum_scatter(core_part, 'a3', scatter_dimension=2, tiled=True)  39.1 us
  transfers between devices with their start and end apart: 7, of which 5 were waited for; matrix products, arithmetic and copies ran while one was open for 6% of the time, Pallas kernels for 0%

commit v1 on v0

v1 whole, which is shorter than its diff:
```python
import functools

import jax
import jax.numpy as jnp
from jax import lax
from jax.experimental import pallas as pl
from jax.experimental.pallas import tpu as pltpu
from jax.sharding import PartitionSpec as P

F32 = jnp.float32
BF16 = jnp.bfloat16
MESH = pl.DeviceIdType.MESH
NN = ((1,), (0,))
NT = ((1,), (1,))
TN = ((0,), (0,))


def dot(a, b, dims=NN):
    return lax.dot_general(a, b, (dims, ((), ())), preferred_element_type=F32)


class Net:
    def __init__(self, send_sem, recv_sem):
        self.send_sem, self.recv_sem, self.copies = send_sem, recv_sem, []

    def send(self, src, dst, device):
        k = len(self.copies)
        copy = pltpu.make_async_remote_copy(
            src_ref=src, dst_ref=dst, send_sem=self.send_sem.at[k], recv_sem=self.recv_sem.at[k], device_id=device, device_id_type=MESH
        )
        copy.start()
        self.copies.append(copy)
        return copy

    def finish(self):
        for copy in self.copies:
            copy.wait_send()


def arrive(copies):
    for copy in copies:
        copy.wait_recv()


def add_slots(buf, count):
    total = buf[0]
    for k in range(1, count):
        total = total + buf[k]
    return total


def swap16(perm, block):
    n = block.shape[-1]
    return dot(perm, block.reshape(256, n)).astype(BF16).reshape(16, 16, n)


def sweep_kernel(
    n1, n2, n3,
    x_hbm, u1_hbm, u2_hbm, u3_hbm,
    new1t_out, p2_out, sq2_out, p3_out, sq3_out, core_out, e_out,
    x, u1, u2, u3, u3_here, new1t, p2, sq2, p3, sq3, out_core, e3,
    perm, u1p, tp, rin, tb, tt, xp, xr, t2,
    y1p, y1y, y1b, y1a, gp1, g1y, g1z, p1y, p1a,
    y2o, y2y, z1, z2, zf, gp2, b0, g0, b1, g1, b2, p2x, p2z, p2c,
    y3p, y3y, y3o, y3z, gp3, c0, h0, c1, h1, c2, p3y, p3x, p3c,
    cp, cpz, e1, e2,
    send_sem, recv_sem, load_sem, store_sem,
):
    me1, me2, me3 = lax.axis_index("a1"), lax.axis_index("a2"), lax.axis_index("a3")
    core, mex, nx = lax.rem(me1, 2), me1 // 2, n1 // 2
    fl, hl, wl = x.shape
    net = Net(send_sem, recv_sem)
    stores = []

    def store(src, dst):
        stores.append(pltpu.make_async_copy(src, dst, store_sem.at[len(stores)]))
        stores[-1].start()


    def peers(me, n):
        return [lax.rem(me + d, n) for d in range(1, n)]

    peers1, peers2, peers3, peersx = peers(me1, n1), peers(me2, n2), peers(me3, n3), peers(mex, nx)

    def share(src, buf, me, ps, device):
        return [net.send(src(p), buf.at[me], device(p)) for p in ps]

    def on1(p):
        return {"a1": p}

    def on2(p):
        return {"a2": p}

    def on3(p):
        return {"a3": p}

    def onx(p):
        return {"a1": 2 * p + core}

    other = {"a1": 2 * mex + 1 - core}

    barrier = pltpu.get_barrier_semaphore()
    for ps, device in ((peers3, on3), (peers2, on2), (peers1, on1)):
        for p in ps:
            pl.semaphore_signal(barrier, inc=1, device_id=device(p), device_id_type=MESH)

    half = fl // 2
    width_here = pl.ds(pl.multiple_of(me3 * wl, wl), wl)
    loads = [
        pltpu.make_async_copy(src, dst, load_sem.at[k])
        for k, (src, dst) in enumerate(
            [
                (u3_hbm.at[width_here], u3_here),
                (x_hbm.at[pl.ds(0, half)], x.at[pl.ds(0, half)]),
                (x_hbm.at[pl.ds(half, half)], x.at[pl.ds(half, half)]),
                (u1_hbm, u1),
                (u2_hbm, u2),
                (u3_hbm, u3),
            ]
        )
    ]
    for load in loads:
        load.start()

    row = lax.broadcasted_iota(jnp.int32, (256, 256), 0)
    col = lax.broadcasted_iota(jnp.int32, (256, 256), 1)
    perm[...] = jnp.where(col == lax.rem(row, 16) * 16 + row // 16, 1.0, 0.0).astype(BF16)

    cz = tp.shape[2]
    reach = n3 // 2
    loads[0].wait()
    u3t = u3_here[...].T.astype(BF16)

    def t_frame(i, carry):
        tp[:, i] = dot(u3t, x[i], NT).reshape(n3, cz, hl)
        return carry

    hops, ch = n3 - 1, cz // 2
    way_step = (1, n3 - 1)

    def t_part(way, sub, root):
        return tp.at[root, pl.ds(sub * half, half), pl.ds(way * ch, ch)]

    def root_at(way, step):
        return lax.rem(me3 + n3 - step, n3) if way == 0 else lax.rem(me3 + step, n3)

    ring = {}

    def send_piece(way, sub, step):
        ring[way, sub, step] = net.send(
            t_part(way, sub, root_at(way, step)), rin.at[way, step - 1, sub], on3(lax.rem(me3 + way_step[way], n3))
        )

    loads[1].wait()
    lax.fori_loop(0, half, t_frame, 0, unroll=4)
    pl.semaphore_wait(barrier, n1 + n2 + n3 - 3)
    send_piece(0, 0, 1)
    send_piece(1, 0, 1)
    loads[2].wait()
    lax.fori_loop(half, fl, t_frame, 0, unroll=4)
    send_piece(0, 1, 1)
    send_piece(1, 1, 1)

    hr = hl // n1

    def x_slice(r):
        for hh in range(0, hr, 16):
            for g in range(0, fl, 16):
                rows = pl.ds(pl.multiple_of(r * hr + hh, 16), 16)
                xp[r, hh : hh + 16, g : g + 16, :] = swap16(perm[...], x[g : g + 16, rows, :])

    frames_here = pl.ds(pl.multiple_of(me1 * fl, fl), fl)
    x_copies = []
    for p in peers1:
        x_slice(p)
        x_copies.append(net.send(xp.at[p], xr.at[:, frames_here, :], on1(p)))
    x_slice(me1)
    xr[:, frames_here, :] = xp[me1]
    for load in loads[3:]:
        load.wait()
    rank1 = u1.shape[0]
    u1p[:, :rank1] = u1[...].T.astype(BF16)
    u1p[:, rank1:] = jnp.zeros((u1p.shape[0], 128 - rank1), BF16)

    for step in range(1, n3):
        for sub in (0, 1):
            for way in (0, 1):
                ring[way, sub, step].wait_recv()
                if step < hops:
                    mine = t_part(way, sub, root_at(way, step + 1))
                    mine[...] = mine[...] + rin[way, step - 1, sub]
                    send_piece(way, sub, step + 1)
    for sub in (0, 1):
        total = [t_part(way, sub, me3)[...] + rin[way, hops - 1, sub] for way in (0, 1)]
        tb[sub * half : (sub + 1) * half] = jnp.concatenate(total, axis=1).astype(BF16)
    for g in range(0, fl, 16):
        tt[:, g : g + 16, :] = swap16(perm[...], tb[g : g + 16])

    u2_here = u2[pl.ds(pl.multiple_of(me2 * hl, hl), hl), :].astype(BF16)
    y1p[...] = dot(tt[...].reshape(cz * fl, hl), u2_here).reshape(y1p.shape)
    cy, c1w = cz // n2, cz // n1
    y1_copies = share(lambda p: y1p.at[pl.ds(p * cy, cy)], y1y, me2, peers2, on2)
    y1y[me2] = y1p[pl.ds(me2 * cy, cy)]
    t_copies = [net.send(tt.at[pl.ds(p * c1w, c1w)], t2.at[:, frames_here, :], on1(p)) for p in peers1]
    t2[:, frames_here, :] = tt[pl.ds(me1 * c1w, c1w)]
    arrive(y1_copies)
    lane = lax.broadcasted_iota(jnp.int32, (cy, fl, 128), 2)
    width = 128 // n2
    y1 = None
    for q in range(n2):
        for side, turn in ((0, 1), (1, n2 - 1)):
            chain = y1y[(q + turn) % n2]
            for k in range(2, n2 + 1):
                chain = chain + y1y[(q + turn * k) % n2]
            y1 = chain if y1 is None else jnp.where(lane >= q * width + side * (width // 2), chain, y1)
    y1 = y1.astype(BF16)
    for c in range(cy):
        y1b[:, c * 128 : (c + 1) * 128] = y1[c]

    y1_all = share(lambda p: y1b, y1a, me1, peers1, on1)
    y1a[me1] = y1b[...]
    arrive(y1_all)
    gp1[...] = dot(y1b[...], y1a[...].reshape(n1 * fl, cy * 128), NT)
    tiles_c = gp1.shape[1] // 128

    def cols_of(p):
        return pl.ds(pl.multiple_of(lax.rem(p, tiles_c) * 128, 128), 128)

    copies = share(lambda p: gp1.at[:, cols_of(p)], g1y, me2, peers2, on2)
    g1y[me2] = gp1[:, cols_of(me2)]
    arrive(copies)
    g1z[me3] = add_slots(g1y, n2)
    arrive(share(lambda p: g1z.at[me3], g1z, me3, peers3, on3))
    gram = add_slots(g1z, n3).astype(BF16)
    p1y[me2] = dot(gram, u1p[cols_of(me2), :])
    arrive(share(lambda p: p1y.at[me2], p1y, me2, peers2, on2))
    p1a[me1] = add_slots(p1y, tiles_c)
    arrive(share(lambda p: p1a.at[me1], p1a, me1, peers1, on1))
    power = p1a[...].reshape(n1 * fl, 128).T[:rank1]
    new1 = power / jnp.sqrt(jnp.sum(power * power, axis=1, keepdims=True))
    new1t[...] = new1
    store(new1t, new1t_out)
    u1t = new1.astype(BF16)

    arrive(t_copies)
    for c in range(c1w):
        y2o[c * rank1 : (c + 1) * rank1] = dot(u1t, t2[c]).astype(BF16)
    y2y[me2] = y2o[...]
    y2_copies = share(lambda p: y2o, y2y, me2, peers2, on2)

    arrive(x_copies)
    for h in range(hr):
        z1[h] = dot(u1t, xr[h]).astype(BF16)
    for hh in range(0, hr, 16):
        for g in range(0, rank1, 16):
            z2[g : g + 16, hh : hh + 16, :] = swap16(perm[...], z1[hh : hh + 16, g : g + 16, :])
    ar = rank1 // n1
    z_rows = pl.ds(pl.multiple_of(me1 * hr, hr), hr)
    z_copies = [net.send(z2.at[pl.ds(p * ar, ar)], zf.at[:, z_rows, :], on1(p)) for p in peers1]
    zf[:, z_rows, :] = z2[pl.ds(me1 * ar, ar)]

    arrive(y2_copies)
    for q in range(n2):
        gp2[:, q] = dot(y2o[...], y2y[q], TN).reshape(2, hl // 2, hl)
    swap = net.send(gp2.at[1 - core], b0, other)
    arrive([swap])
    g0[...] = (gp2[core] + b0[...]).reshape(g0.shape)
    pieces2 = []
    parts = hl // 2 // n3 // 8
    for k in range(parts):
        b1[k, mex] = g0[mex, :, k]
        pieces_x = share(lambda p: g0.at[p, :, k], b1.at[k], mex, peersx, onx)
        pieces2.append(pieces_x)
    pieces_z = []
    for k in range(parts):
        arrive(pieces2[k])
        g1[:, k] = add_slots(b1.at[k], nx)
        pieces_z += share(lambda p: g1.at[p, k], b2.at[k], me3, peers3, on3)
        b2[k, me3] = g1[me3, k]
    arrive(pieces_z)
    gram = jnp.concatenate([add_slots(b2.at[k], n3) for k in range(parts)], axis=0).astype(BF16)
    p2x[mex] = dot(gram, u2[pl.ds(pl.multiple_of(mex * hl, hl), hl), :].astype(BF16))
    arrive(share(lambda p: p2x.at[mex], p2x, mex, peersx, onx))
    p2z[me3] = add_slots(p2x, nx)
    arrive(share(lambda p: p2z.at[me3], p2z, me3, peers3, on3))
    p2c[core] = p2z[...].reshape(hl // 2, 128)
    arrive([net.send(p2c.at[core], p2c.at[core], other)])
    power = p2c[...].reshape(hl, 128)
    sq2[me2] = jnp.broadcast_to(jnp.sum(power * power, axis=0, keepdims=True), (8, 128))
    p2[...] = power
    store(p2, p2_out.at[me2])
    copies = share(lambda p: sq2.at[me2], sq2, me2, peers2, on2)
    arrive(copies)
    store(sq2, sq2_out)
    norm2 = jnp.sqrt(add_slots(sq2, n2)[:1])
    u2t = (power / norm2).T.astype(BF16)

    arrive(z_copies)
    bq = 128 // n2
    for a in range(ar):
        y3p[:, a] = dot(u2t, zf[a]).reshape(n2, bq, wl)
    copies = share(lambda p: y3p.at[p], y3y, me2, peers2, on2)
    p2_copies = share(lambda p: p2, p2_out, me2, peers2, on2)
    y3y[me2] = y3p[me2]
    arrive(copies)
    y3o[...] = add_slots(y3y, n2).astype(BF16).reshape(ar * bq, wl)

    wx = wl // 2 // nx
    order = [d for k in range(1, reach) for d in (k, n3 - k)] + [reach]
    peer_of = {d: lax.rem(me3 + d, n3) for d in order}
    y3z[me3] = y3o[...]
    incoming = {n3 - d: net.send(y3o, y3z.at[me3], on3(peer_of[d])) for d in order}
    groups = [[0, 1, n3 - 1], [2, n3 - 2], [3, n3 - 3, 4]]
    pieces_x = []
    for group in groups:
        swaps = []
        for d in group:
            if d:
                arrive([incoming[d]])
            q = peer_of[d] if d else me3
            gp3[:, q] = dot(y3o[...], y3z[q], TN).reshape(2, wl // 2, wl)
            swaps.append((q, net.send(gp3.at[1 - core, q], c0.at[q], other)))
        for q, swap in swaps:
            arrive([swap])
            h0[:, q] = (gp3[core, q] + c0[q]).reshape(nx, wx, wl)
            c1[mex, q] = h0[mex, q]
            pieces_x += [net.send(h0.at[p, q], c1.at[mex, q], onx(p)) for p in peersx]
    arrive(pieces_x)
    h1[...] = add_slots(c1, nx)
    zq = n3 // n2
    copies = share(lambda p: h1.at[pl.ds(p * zq, zq)], c2, me2, peers2, on2)
    c2[me2] = h1[pl.ds(me2 * zq, zq)]
    arrive(copies)
    gram = add_slots(c2, n2).astype(BF16)
    power = jnp.zeros((wx, 128), F32)
    for q in range(zq):
        power = power + dot(gram[q], u3[pl.ds(pl.multiple_of((me2 * zq + q) * wl, wl), wl), :].astype(BF16))
    p3y[me2] = power
    arrive(share(lambda p: p3y.at[me2], p3y, me2, peers2, on2))
    p3x[mex] = add_slots(p3y, n2)
    arrive(share(lambda p: p3x.at[mex], p3x, mex, peersx, onx))
    p3c[core] = p3x[...].reshape(wl // 2, 128)
    arrive([net.send(p3c.at[core], p3c.at[core], other)])
    power = p3c[...].reshape(wl, 128)
    sq3[me3] = jnp.broadcast_to(jnp.sum(power * power, axis=0, keepdims=True), (8, 128))
    p3[...] = power
    store(p3, p3_out.at[me3])
    copies = share(lambda p: sq3.at[me3], sq3, me3, peers3, on3)
    arrive(copies)
    store(sq3, sq3_out)
    norm3 = jnp.sqrt(add_slots(sq3, n3)[:1])
    u3n = (power / norm3).T.astype(BF16)

    kk = ar * bq
    cp[...] = jnp.zeros_like(cp)
    cp[:, :, :kk] = dot(u3n, y3o[...], NT).reshape(n3, cz, kk)
    copies = share(lambda p: cp.at[p], cpz, me3, peers3, on3)
    p3_copies = share(lambda p: p3, p3_out, me3, peers3, on3)
    cpz[me3] = cp[me3]
    arrive(copies)
    total = add_slots(cpz, n3)
    out_core[...] = total
    store(out_core, core_out)
    e1[me1] = jnp.broadcast_to(jnp.sum(total * total, axis=(0, 1), keepdims=True), (8, 128))
    arrive(share(lambda p: e1.at[me1], e1, me1, peers1, on1))
    e2[me2] = add_slots(e1, n1)
    arrive(share(lambda p: e2.at[me2], e2, me2, peers2, on2))
    e3[me3] = add_slots(e2, n2)
    arrive(share(lambda p: e3.at[me3], e3, me3, peers3, on3))
    store(e3, e_out)
    arrive(p2_copies + p3_copies)
    net.finish()
    for copy in stores:
        copy.wait()


def finish_kernel(raws, outs, ins, results, in_sem, out_sem):
    loads = [pltpu.make_async_copy(src, dst, in_sem.at[k]) for k, (src, dst) in enumerate(zip(raws, ins))]
    for load in loads:
        load.start()
    new1t, p2, sq2, p3, sq3, core_t, e3 = ins
    out2, out3, out_core, out_e = results
    finals = [pltpu.make_async_copy(src, dst, out_sem.at[k]) for k, (src, dst) in enumerate(zip((new1t,) + results, outs))]
    loads[1].wait()
    loads[2].wait()
    out2[...] = p2[...].reshape(out2.shape) / jnp.sqrt(add_slots(sq2, sq2.shape[0])[:1])
    finals[1].start()
    loads[3].wait()
    loads[4].wait()
    out3[...] = p3[...].reshape(out3.shape) / jnp.sqrt(add_slots(sq3, sq3.shape[0])[:1])
    finals[2].start()
    loads[0].wait()
    finals[0].start()
    loads[5].wait()
    width = out_core.shape[2]
    for a in range(out_core.shape[0]):
        out_core[a] = core_t[:, a * width : (a + 1) * width]
    finals[3].start()
    loads[6].wait()
    out_e[...] = add_slots(e3, e3.shape[0])[:1, :1]
    finals[4].start()
    for final in finals:
        final.wait()


def solution(mesh):
    n1, n2, n3 = mesh.shape["a1"], mesh.shape["a2"], mesh.shape["a3"]
    nx = n1 // 2

    def local_sweep(tensor, u_time, u_height, u_width):
        fl, hl, wl = tensor.shape
        rank1 = u_time.shape[1]
        half, cz, cy, c1w, hr = fl // 2, 128 // n3, 128 // n3 // n2, 128 // n3 // n1, hl // n1
        ar, bq, wx, zq = rank1 // n1, 128 // n2, wl // 2 // nx, n3 // n2
        hops = n3 - 1
        frames, parts = n1 * fl, hl // 2 // n3 // 8
        outs = [(rank1, frames), (hl, 128), (n2, 8, 128), (wl, 128), (n3, 8, 128), (cz, 256), (n3, 8, 128)]
        scratch = [
            (tensor.shape, BF16), ((rank1, frames), F32), (u_height.shape, F32), (u_width.shape, F32), ((wl, 128), F32), *[(shape, F32) for shape in outs],
            ((256, 256), BF16), ((frames, 128), BF16), ((n3, fl, cz, hl), F32), ((2, hops, 2, half, cz // 2, hl), F32),
            ((fl, cz, hl), BF16), ((cz, fl, hl), BF16), ((n1, hr, fl, wl), BF16), ((hr, frames, wl), BF16), ((c1w, frames, hl), BF16),
            ((cz, fl, 128), F32), ((n2, cy, fl, 128), F32), ((fl, cy * 128), BF16), ((n1, fl, cy * 128), BF16), ((fl, frames), F32),
            ((n2, fl, 128), F32), ((n3, fl, 128), F32), ((n2, fl, 128), F32), ((n1, fl, 128), F32),
            ((c1w * rank1, hl), BF16), ((n2, c1w * rank1, hl), BF16), ((hr, rank1, wl), BF16), ((rank1, hr, wl), BF16), ((ar, hl, wl), BF16),
            ((2, n2, hl // 2, hl), F32), ((n2, hl // 2, hl), F32), ((n2, n3, parts, 8, hl), F32), ((parts, nx, n3, 8, hl), F32),
            ((n3, parts, 8, hl), F32), ((parts, n3, 8, hl), F32),
            ((nx, hl // 2 // n3, 128), F32), ((n3, hl // 2 // n3, 128), F32), ((2, hl // 2, 128), F32),
            ((n2, ar, bq, wl), F32), ((n2, ar, bq, wl), F32), ((ar * bq, wl), BF16), ((n3, ar * bq, wl), BF16),
            ((2, n3, wl // 2, wl), F32), ((n3, wl // 2, wl), F32), ((nx, n3, wx, wl), F32), ((nx, n3, wx, wl), F32),
            ((n3, wx, wl), F32), ((n2, zq, wx, wl), F32),
            ((n2, wx, 128), F32), ((nx, wx, 128), F32), ((2, wl // 2, 128), F32),
            ((n3, cz, 256), F32), ((n3, cz, 256), F32), ((n1, 8, 128), F32), ((n2, 8, 128), F32),
        ]
        raws = list(outs)
        raws[1], raws[3] = (n2, hl, 128), (n3, wl, 128)
        raw = pl.pallas_call(
            functools.partial(sweep_kernel, n1, n2, n3),
            out_shape=[jax.ShapeDtypeStruct(shape, F32) for shape in raws],
            in_specs=[pl.BlockSpec(memory_space=pl.ANY)] * 4,
            out_specs=[pl.BlockSpec(memory_space=pl.ANY)] * 7,
            scratch_shapes=[pltpu.VMEM(shape, dtype) for shape, dtype in scratch]
            + [pltpu.SemaphoreType.DMA((256,)), pltpu.SemaphoreType.DMA((256,)), pltpu.SemaphoreType.DMA((6,)), pltpu.SemaphoreType.DMA((8,))],
            compiler_params=pltpu.CompilerParams(collective_id=0, has_side_effects=True, vmem_limit_bytes=60 * 1024 * 1024),
            name="sweep",
        )(tensor, u_time.T, u_height, u_width)
        shapes = [(rank1, frames), u_height.shape, u_width.shape, (ar, cz, bq), (1, 1)]
        new1t, new2, new3, core_t, energy = pl.pallas_call(
            lambda *refs: finish_kernel(refs[:7], refs[7:12], refs[12:19], refs[19:23], *refs[23:]),
            out_shape=[jax.ShapeDtypeStruct(shape, F32) for shape in shapes],
            in_specs=[pl.BlockSpec(memory_space=pl.ANY)] * 7,
            out_specs=[pl.BlockSpec(memory_space=pl.ANY)] * 5,
            scratch_shapes=[pltpu.VMEM(shape, F32) for shape in raws + shapes[1:]]
            + [pltpu.SemaphoreType.DMA((7,)), pltpu.SemaphoreType.DMA((5,))],
            compiler_params=pltpu.CompilerParams(vmem_limit_bytes=60 * 1024 * 1024),
            name="finish",
        )(*raw)
        return new1t.T, new2, new3, core_t.transpose(0, 2, 1), energy.reshape(())

    return jax.shard_map(
        local_sweep,
        mesh=mesh,
        in_specs=(P("a1", "a2", "a3"), P(), P(), P()),
        out_specs=(P(), P(), P(), P("a1", "a2", "a3"), P()),
        check_vma=False,
    )
```

time: 1010 us -> 202 us (0.20)
  blocking collectives: 774 us -> 0 us
  Pallas kernels: 0 us -> 202 us
  waiting for transfers between devices: 181 us -> 0 us
  local copies, waits for them, and re-layouts: 15.6 us -> 0 us
  between operations: 14.6 us -> 0.64 us
  matrix products: 13.4 us -> 0 us
    psum x7 -> x0, blocking collectives: 631 us -> none  [the longest x3 492 us: gram_update(): gram_rows = lax.psum(gram_part, sum_axes).astype(jnp.bfloat16)]
    pallas_call x0 -> x2, Pallas kernels: none -> 202 us  [the longest x1 199 us: local_sweep(): pl.pallas_call(functools.partial(sweep_kernel, n1, n2, n3), out_shape=[ja...]
    reduce_scatter x5 -> x0, waiting for transfers between devices: 168 us -> none  [the longest x1 78.8 us: local_sweep(): lax.psum_scatter(t_part.reshape(frames, grid_h, -1), 'a3', scatter_dimens...]
    all_gather x6 -> x0, blocking collectives: 89.4 us -> none  [the longest x3 46.4 us: gram_update(): all_rows = lax.all_gather(local_rows, row_axes, axis=0, tiled=True)]
    unnamed x1 -> x0, blocking collectives: 53 us -> none
    dot_general x12 -> x0, matrix products: 13.4 us -> none  [the longest x1 5.27 us: local_sweep(): lax.dot_general(time_rows, tensor.reshape(frames, grid_h * grid_w), (((0,...]
    unnamed x7 -> x0, waiting for transfers between devices: 13.1 us -> none
    unnamed x20 -> x0, local copies, waits for them, and re-layouts: 12.4 us -> none
  transfers between devices with their start and end apart: 7 -> 0, of which waited for: 5 -> 0; matrix products, arithmetic and copies ran while one was open for 6% -> 0% of each run, Pallas kernels for 0% -> 0%
where the time goes in v1:
time: 202 us
  Pallas kernels  202 us (100%)
    pallas_call x1, Pallas kernels, local_sweep(): pl.pallas_call(functools.partial(sweep_kernel, n1, n2, n3), out_shape=[ja...  199 us

profile of v1, /device:TPU:1, one launch (start us, length us, event | category | flops | bytes accessed | tf_op | source)
XLA Modules:
  0.0 202.2 jit_solution(13241348013554954276)
XLA Ops:
  0.6 199.4 %sweep.1 = (f32[48,384]{1,0:T(8,128)}, f32[4,256,128]{2,1,0:T(8,128)}, f32[4,8,128]{2,1,0:T(8,128)}, f32[8,128,128]{2,1,0:T(8,128)}, f32[8,8,128]{2,1,0:T(8,128)...) custom-call(bf16[48,256,128]{2,1,0:T(8,128)(2,1)} %x_hbm.1, f32[48,384]{1,0:T(8,128)} %bitcast.4, f32[1024,128]{1,0:T(8,128)} %u2_hbm.1, ...), custom_call_target="tpu_custom_call" | custom-call | tf_op jit(solution)/shard_map/sweep/pallas_call | solution.py:436
  200.0 2.2 %finish.1 = (f32[48,384]{1,0:T(8,128)}, f32[1024,128]{1,0:T(8,128)}, f32[1024,128]{1,0:T(8,128)}, f32[6,16,32]{2,1,0:T(8,128)}, f32[1,1]{1,0:T(1,128)}) custom-call(f32[48,384]{1,0:T(8,128)} %get-tuple-element.17.refs_0_, f32[4,256,128]{2,1,0:T(8,128)} %get-tuple-element.18.refs_1_, f32[4,8,128]{2,1,0:T(8,128)} %get-tuple-element.19.refs_2_, ...), custom_call_target="tpu_custom_call" | custom-call | tf_op jit(solution)/shard_map/finish/pallas_call | solution.py:447

commit v2 on v1

--- a/solution.py
+++ b/solution.py
@@ -10,6 +10,7 @@
 F32 = jnp.float32
 BF16 = jnp.bfloat16
 MESH = pl.DeviceIdType.MESH
+EXCHANGES = 82
 NN = ((1,), (0,))
 NT = ((1,), (1,))
 TN = ((0,), (0,))
@@ -20,26 +21,32 @@
 
 
 class Net:
-    def __init__(self, send_sem, recv_sem):
-        self.send_sem, self.recv_sem, self.copies = send_sem, recv_sem, []
-
-    def send(self, src, dst, device):
-        k = len(self.copies)
-        copy = pltpu.make_async_remote_copy(
+    def __init__(self, send_sem, recv_sem, near):
+        self.send_sem, self.recv_sem, self.near, self.exchanges = send_sem, recv_sem, near, []
+
+    def describe(self, k, src, dst, device):
+        return pltpu.make_async_remote_copy(
             src_ref=src, dst_ref=dst, send_sem=self.send_sem.at[k], recv_sem=self.recv_sem.at[k], device_id=device, device_id_type=MESH
         )
-        copy.start()
-        self.copies.append(copy)
-        return copy
+
+    def exchange(self, copies, span):
+        k = len(self.exchanges)
+        for src, dst, device in copies:
+            self.describe(k, src, dst, device).start()
+        self.exchanges.append(self.describe(k, span, span, self.near))
+        return self.exchanges[-1]
+
+    def send(self, src, dst, device):
+        return self.exchange([(src, dst, device)], dst)
 
     def finish(self):
-        for copy in self.copies:
-            copy.wait_send()
-
-
-def arrive(copies):
-    for copy in copies:
-        copy.wait_recv()
+        for exchange in self.exchanges:
+            exchange.wait_send()
+
+
+def arrive(exchanges):
+    for exchange in exchanges:
+        exchange.wait_recv()
 
 
 def add_slots(buf, count):
@@ -59,17 +66,17 @@
     x_hbm, u1_hbm, u2_hbm, u3_hbm,
     new1t_out, p2_out, sq2_out, p3_out, sq3_out, core_out, e_out,
     x, u1, u2, u3, u3_here, new1t, p2, sq2, p3, sq3, out_core, e3,
-    perm, u1p, tp, rin, tb, tt, xp, xr, t2,
+    perm, u1p, tp, rin, rin_b, tb, tt, xp, xr, t2,
     y1p, y1y, y1b, y1a, gp1, g1y, g1z, p1y, p1a,
     y2o, y2y, z1, z2, zf, gp2, b0, g0, b1, g1, b2, p2x, p2z, p2c,
     y3p, y3y, y3o, y3z, gp3, c0, h0, c1, h1, c2, p3y, p3x, p3c,
-    cp, cpz, e1, e2,
+    cp, cpz, e1,
     send_sem, recv_sem, load_sem, store_sem,
 ):
     me1, me2, me3 = lax.axis_index("a1"), lax.axis_index("a2"), lax.axis_index("a3")
     core, mex, nx = lax.rem(me1, 2), me1 // 2, n1 // 2
     fl, hl, wl = x.shape
-    net = Net(send_sem, recv_sem)
+    net = Net(send_sem, recv_sem, {"a3": lax.rem(me3 + 1, n3)})
     stores = []
 
     def store(src, dst):
@@ -83,7 +90,7 @@
     peers1, peers2, peers3, peersx = peers(me1, n1), peers(me2, n2), peers(me3, n3), peers(mex, nx)
 
     def share(src, buf, me, ps, device):
-        return [net.send(src(p), buf.at[me], device(p)) for p in ps]
+        return [net.exchange([(src(p), buf.at[me], device(p)) for p in ps], buf.at[pl.ds(0, len(ps))])]
 
     def on1(p):
         return {"a1": p}
@@ -104,7 +111,7 @@
         for p in ps:
             pl.semaphore_signal(barrier, inc=1, device_id=device(p), device_id_type=MESH)
 
-    half = fl // 2
+    half = fl // 3 * 2
     width_here = pl.ds(pl.multiple_of(me3 * wl, wl), wl)
     loads = [
         pltpu.make_async_copy(src, dst, load_sem.at[k])
@@ -112,7 +119,7 @@
             [
                 (u3_hbm.at[width_here], u3_here),
                 (x_hbm.at[pl.ds(0, half)], x.at[pl.ds(0, half)]),
-                (x_hbm.at[pl.ds(half, half)], x.at[pl.ds(half, half)]),
+                (x_hbm.at[pl.ds(half, fl - half)], x.at[pl.ds(half, fl - half)]),
                 (u1_hbm, u1),
                 (u2_hbm, u2),
                 (u3_hbm, u3),
@@ -122,6 +129,10 @@
     for load in loads:
         load.start()
 
+    for p in peers2:
+        for q in peers1:
+            pl.semaphore_signal(barrier, inc=1, device_id={"a2": p, "a1": q}, device_id_type=MESH)
+
     row = lax.broadcasted_iota(jnp.int32, (256, 256), 0)
     col = lax.broadcasted_iota(jnp.int32, (256, 256), 1)
     perm[...] = jnp.where(col == lax.rem(row, 16) * 16 + row // 16, 1.0, 0.0).astype(BF16)
@@ -136,10 +147,12 @@
         return carry
 
     hops, ch = n3 - 1, cz // 2
+    cuts = ((0, half), (half, fl - half))
+    rins = (rin, rin_b)
     way_step = (1, n3 - 1)
 
     def t_part(way, sub, root):
-        return tp.at[root, pl.ds(sub * half, half), pl.ds(way * ch, ch)]
+        return tp.at[root, pl.ds(*cuts[sub]), pl.ds(way * ch, ch)]
 
     def root_at(way, step):
         return lax.rem(me3 + n3 - step, n3) if way == 0 else lax.rem(me3 + step, n3)
@@ -148,12 +161,12 @@
 
     def send_piece(way, sub, step):
         ring[way, sub, step] = net.send(
-            t_part(way, sub, root_at(way, step)), rin.at[way, step - 1, sub], on3(lax.rem(me3 + way_step[way], n3))
+            t_part(way, sub, root_at(way, step)), rins[sub].at[way, step - 1], on3(lax.rem(me3 + way_step[way], n3))
         )
 
     loads[1].wait()
     lax.fori_loop(0, half, t_frame, 0, unroll=4)
-    pl.semaphore_wait(barrier, n1 + n2 + n3 - 3)
+    pl.semaphore_wait(barrier, n1 * n2 + n3 - 2)
     send_piece(0, 0, 1)
     send_piece(1, 0, 1)
     loads[2].wait()
@@ -170,10 +183,12 @@
                 xp[r, hh : hh + 16, g : g + 16, :] = swap16(perm[...], x[g : g + 16, rows, :])
 
     frames_here = pl.ds(pl.multiple_of(me1 * fl, fl), fl)
-    x_copies = []
-    for p in peers1:
-        x_slice(p)
-        x_copies.append(net.send(xp.at[p], xr.at[:, frames_here, :], on1(p)))
+    def x_moves():
+        for p in peers1:
+            x_slice(p)
+            yield xp.at[p], xr.at[:, frames_here, :], on1(p)
+
+    x_copies = [net.exchange(x_moves(), xr.at[:, pl.ds(0, (n1 - 1) * fl), :])]
     x_slice(me1)
     xr[:, frames_here, :] = xp[me1]
     for load in loads[3:]:
@@ -182,26 +197,34 @@
     u1p[:, :rank1] = u1[...].T.astype(BF16)
     u1p[:, rank1:] = jnp.zeros((u1p.shape[0], 128 - rank1), BF16)
 
+    u2_here = u2[pl.ds(pl.multiple_of(me2 * hl, hl), hl), :].astype(BF16)
+    cy, c1w = cz // n2, cz // n1
+    y1_copies = []
+
+    def t_done(sub):
+        first, count = cuts[sub]
+        total = [t_part(way, sub, me3)[...] + rins[sub][way, hops - 1] for way in (0, 1)]
+        tb[first : first + count] = jnp.concatenate(total, axis=1).astype(BF16)
+        for g in range(first, first + count, 16):
+            tt[:, g : g + 16, :] = swap16(perm[...], tb[g : g + 16])
+        frames = pl.ds(first, count)
+        y1p[:, frames, :] = dot(tt[:, frames, :].reshape(cz * count, hl), u2_here).reshape(cz, count, 128)
+        moves = [(y1p.at[pl.ds(p * cy, cy), frames], y1y.at[me2, :, frames], on2(p)) for p in peers2]
+        y1_copies.append(net.exchange(moves, y1y.at[pl.ds(0, n2 - 1), :, frames]))
+        y1y[me2, :, frames] = y1p[pl.ds(me2 * cy, cy), frames]
+
     for step in range(1, n3):
         for sub in (0, 1):
             for way in (0, 1):
-                ring[way, sub, step].wait_recv()
+                arrive([ring[way, sub, step]])
                 if step < hops:
                     mine = t_part(way, sub, root_at(way, step + 1))
-                    mine[...] = mine[...] + rin[way, step - 1, sub]
+                    mine[...] = mine[...] + rins[sub][way, step - 1]
                     send_piece(way, sub, step + 1)
-    for sub in (0, 1):
-        total = [t_part(way, sub, me3)[...] + rin[way, hops - 1, sub] for way in (0, 1)]
-        tb[sub * half : (sub + 1) * half] = jnp.concatenate(total, axis=1).astype(BF16)
-    for g in range(0, fl, 16):
-        tt[:, g : g + 16, :] = swap16(perm[...], tb[g : g + 16])
-
-    u2_here = u2[pl.ds(pl.multiple_of(me2 * hl, hl), hl), :].astype(BF16)
-    y1p[...] = dot(tt[...].reshape(cz * fl, hl), u2_here).reshape(y1p.shape)
-    cy, c1w = cz // n2, cz // n1
-    y1_copies = share(lambda p: y1p.at[pl.ds(p * cy, cy)], y1y, me2, peers2, on2)
-    y1y[me2] = y1p[pl.ds(me2 * cy, cy)]
-    t_copies = [net.send(tt.at[pl.ds(p * c1w, c1w)], t2.at[:, frames_here, :], on1(p)) for p in peers1]
+            if step == hops:
+                t_done(sub)
+    t_moves = [(tt.at[pl.ds(p * c1w, c1w)], t2.at[:, frames_here, :], on1(p)) for p in peers1]
+    t_copies = [net.exchange(t_moves, t2.at[:, pl.ds(0, (n1 - 1) * fl), :])]
     t2[:, frames_here, :] = tt[pl.ds(me1 * c1w, c1w)]
     arrive(y1_copies)
     lane = lax.broadcasted_iota(jnp.int32, (cy, fl, 128), 2)
@@ -256,7 +279,8 @@
             z2[g : g + 16, hh : hh + 16, :] = swap16(perm[...], z1[hh : hh + 16, g : g + 16, :])
     ar = rank1 // n1
     z_rows = pl.ds(pl.multiple_of(me1 * hr, hr), hr)
-    z_copies = [net.send(z2.at[pl.ds(p * ar, ar)], zf.at[:, z_rows, :], on1(p)) for p in peers1]
+    z_moves = [(z2.at[pl.ds(p * ar, ar)], zf.at[:, z_rows, :], on1(p)) for p in peers1]
+    z_copies = [net.exchange(z_moves, zf.at[:, pl.ds(0, (n1 - 1) * hr), :])]
     zf[:, z_rows, :] = z2[pl.ds(me1 * ar, ar)]
 
     arrive(y2_copies)
@@ -324,7 +348,7 @@
             arrive([swap])
             h0[:, q] = (gp3[core, q] + c0[q]).reshape(nx, wx, wl)
             c1[mex, q] = h0[mex, q]
-            pieces_x += [net.send(h0.at[p, q], c1.at[mex, q], onx(p)) for p in peersx]
+            pieces_x.append(net.exchange([(h0.at[p, q], c1.at[mex, q], onx(p)) for p in peersx], c1.at[pl.ds(0, nx - 1), 0]))
     arrive(pieces_x)
     h1[...] = add_slots(c1, nx)
     zq = n3 // n2
@@ -361,11 +385,15 @@
     total = add_slots(cpz, n3)
     out_core[...] = total
     store(out_core, core_out)
-    e1[me1] = jnp.broadcast_to(jnp.sum(total * total, axis=(0, 1), keepdims=True), (8, 128))
-    arrive(share(lambda p: e1.at[me1], e1, me1, peers1, on1))
-    e2[me2] = add_slots(e1, n1)
-    arrive(share(lambda p: e2.at[me2], e2, me2, peers2, on2))
-    e3[me3] = add_slots(e2, n2)
+    mine = me2 * n1 + me1
+    e1[mine] = jnp.broadcast_to(jnp.sum(total * total, axis=(0, 1), keepdims=True), (8, 128))
+    e_moves = []
+    for d2 in range(n2):
+        for d1 in range(n1):
+            if d1 or d2:
+                e_moves.append((e1.at[mine], e1.at[mine], {"a2": lax.rem(me2 + d2, n2), "a1": lax.rem(me1 + d1, n1)}))
+    arrive([net.exchange(e_moves, e1.at[pl.ds(0, n1 * n2 - 1)])])
+    e3[me3] = add_slots(e1, n1 * n2)
     arrive(share(lambda p: e3.at[me3], e3, me3, peers3, on3))
     store(e3, e_out)
     arrive(p2_copies + p3_copies)
@@ -410,14 +438,14 @@
     def local_sweep(tensor, u_time, u_height, u_width):
         fl, hl, wl = tensor.shape
         rank1 = u_time.shape[1]
-        half, cz, cy, c1w, hr = fl // 2, 128 // n3, 128 // n3 // n2, 128 // n3 // n1, hl // n1
+        half, cz, cy, c1w, hr = fl // 3 * 2, 128 // n3, 128 // n3 // n2, 128 // n3 // n1, hl // n1
         ar, bq, wx, zq = rank1 // n1, 128 // n2, wl // 2 // nx, n3 // n2
         hops = n3 - 1
         frames, parts = n1 * fl, hl // 2 // n3 // 8
         outs = [(rank1, frames), (hl, 128), (n2, 8, 128), (wl, 128), (n3, 8, 128), (cz, 256), (n3, 8, 128)]
         scratch = [
             (tensor.shape, BF16), ((rank1, frames), F32), (u_height.shape, F32), (u_width.shape, F32), ((wl, 128), F32), *[(shape, F32) for shape in outs],
-            ((256, 256), BF16), ((frames, 128), BF16), ((n3, fl, cz, hl), F32), ((2, hops, 2, half, cz // 2, hl), F32),
+            ((256, 256), BF16), ((frames, 128), BF16), ((n3, fl, cz, hl), F32), ((2, hops, half, cz // 2, hl), F32), ((2, hops, fl - half, cz // 2, hl), F32),
             ((fl, cz, hl), BF16), ((cz, fl, hl), BF16), ((n1, hr, fl, wl), BF16), ((hr, frames, wl), BF16), ((c1w, frames, hl), BF16),
             ((cz, fl, 128), F32), ((n2, cy, fl, 128), F32), ((fl, cy * 128), BF16), ((n1, fl, cy * 128), BF16), ((fl, frames), F32),
             ((n2, fl, 128), F32), ((n3, fl, 128), F32), ((n2, fl, 128), F32), ((n1, fl, 128), F32),
@@ -429,7 +457,7 @@
             ((2, n3, wl // 2, wl), F32), ((n3, wl // 2, wl), F32), ((nx, n3, wx, wl), F32), ((nx, n3, wx, wl), F32),
             ((n3, wx, wl), F32), ((n2, zq, wx, wl), F32),
             ((n2, wx, 128), F32), ((nx, wx, 128), F32), ((2, wl // 2, 128), F32),
-            ((n3, cz, 256), F32), ((n3, cz, 256), F32), ((n1, 8, 128), F32), ((n2, 8, 128), F32),
+            ((n3, cz, 256), F32), ((n3, cz, 256), F32), ((n2 * n1, 8, 128), F32),
         ]
         raws = list(outs)
         raws[1], raws[3] = (n2, hl, 128), (n3, wl, 128)
@@ -439,7 +467,7 @@
             in_specs=[pl.BlockSpec(memory_space=pl.ANY)] * 4,
             out_specs=[pl.BlockSpec(memory_space=pl.ANY)] * 7,
             scratch_shapes=[pltpu.VMEM(shape, dtype) for shape, dtype in scratch]
-            + [pltpu.SemaphoreType.DMA((256,)), pltpu.SemaphoreType.DMA((256,)), pltpu.SemaphoreType.DMA((6,)), pltpu.SemaphoreType.DMA((8,))],
+            + [pltpu.SemaphoreType.DMA((EXCHANGES,)), pltpu.SemaphoreType.DMA((EXCHANGES,)), pltpu.SemaphoreType.DMA((6,)), pltpu.SemaphoreType.DMA((7,))],
             compiler_params=pltpu.CompilerParams(collective_id=0, has_side_effects=True, vmem_limit_bytes=60 * 1024 * 1024),
             name="sweep",
         )(tensor, u_time.T, u_height, u_width)

time: 202 us -> 200 us (0.990)
  Pallas kernels: 202 us -> 199 us
    pallas_call x1, Pallas kernels: 199 us -> 197 us  [local_sweep(): pl.pallas_call(functools.partial(sweep_kernel, n1, n2, n3), out_shape=[ja...]
where the time goes in v2:
time: 200 us
  Pallas kernels  199 us (100%)
    pallas_call x1, Pallas kernels, local_sweep(): pl.pallas_call(functools.partial(sweep_kernel, n1, n2, n3), out_shape=[ja...  197 us

profile of v2, /device:TPU:1, one launch (start us, length us, event | category | flops | bytes accessed | tf_op | source)
XLA Modules:
  0.0 200.0 jit_solution(3823936777452222336)
XLA Ops:
  0.6 197.1 %sweep.1 = (f32[48,384]{1,0:T(8,128)}, f32[4,256,128]{2,1,0:T(8,128)}, f32[4,8,128]{2,1,0:T(8,128)}, f32[8,128,128]{2,1,0:T(8,128)}, f32[8,8,128]{2,1,0:T(8,128)...) custom-call(bf16[48,256,128]{2,1,0:T(8,128)(2,1)} %x_hbm.1, f32[48,384]{1,0:T(8,128)} %bitcast.4, f32[1024,128]{1,0:T(8,128)} %u2_hbm.1, ...), custom_call_target="tpu_custom_call" | custom-call | tf_op jit(solution)/shard_map/sweep/pallas_call | solution.py:464
  197.8 2.2 %finish.1 = (f32[48,384]{1,0:T(8,128)}, f32[1024,128]{1,0:T(8,128)}, f32[1024,128]{1,0:T(8,128)}, f32[6,16,32]{2,1,0:T(8,128)}, f32[1,1]{1,0:T(1,128)}) custom-call(f32[48,384]{1,0:T(8,128)} %get-tuple-element.17.refs_0_, f32[4,256,128]{2,1,0:T(8,128)} %get-tuple-element.18.refs_1_, f32[4,8,128]{2,1,0:T(8,128)} %get-tuple-element.19.refs_2_, ...), custom_call_target="tpu_custom_call" | custom-call | tf_op jit(solution)/shard_map/finish/pallas_call | solution.py:475

commit v3 on v2

--- a/solution.py
+++ b/solution.py
@@ -10,7 +10,7 @@
 F32 = jnp.float32
 BF16 = jnp.bfloat16
 MESH = pl.DeviceIdType.MESH
-EXCHANGES = 82
+EXCHANGES = 83
 NN = ((1,), (0,))
 NT = ((1,), (1,))
 TN = ((0,), (0,))
@@ -65,7 +65,7 @@
     n1, n2, n3,
     x_hbm, u1_hbm, u2_hbm, u3_hbm,
     new1t_out, p2_out, sq2_out, p3_out, sq3_out, core_out, e_out,
-    x, u1, u2, u3, u3_here, new1t, p2, sq2, p3, sq3, out_core, e3,
+    x, u1, u2, u3, u3_here, new1t, p2, sq2, sq3, out_core, e3,
     perm, u1p, tp, rin, rin_b, tb, tt, xp, xr, t2,
     y1p, y1y, y1b, y1a, gp1, g1y, g1z, p1y, p1a,
     y2o, y2y, z1, z2, zf, gp2, b0, g0, b1, g1, b2, p2x, p2z, p2c,
@@ -367,8 +367,7 @@
     arrive([net.send(p3c.at[core], p3c.at[core], other)])
     power = p3c[...].reshape(wl, 128)
     sq3[me3] = jnp.broadcast_to(jnp.sum(power * power, axis=0, keepdims=True), (8, 128))
-    p3[...] = power
-    store(p3, p3_out.at[me3])
+    store(p3c, p3_out.at[me3])
     copies = share(lambda p: sq3.at[me3], sq3, me3, peers3, on3)
     arrive(copies)
     store(sq3, sq3_out)
@@ -379,7 +378,8 @@
     cp[...] = jnp.zeros_like(cp)
     cp[:, :, :kk] = dot(u3n, y3o[...], NT).reshape(n3, cz, kk)
     copies = share(lambda p: cp.at[p], cpz, me3, peers3, on3)
-    p3_copies = share(lambda p: p3, p3_out, me3, peers3, on3)
+    p3_moves = [(p3c.at[core], p3_out.at[me3, core], on3(p)) for p in peers3]
+    p3_half = net.exchange(p3_moves, p3_out.at[pl.ds(0, n3 - 1), 0])
     cpz[me3] = cp[me3]
     arrive(copies)
     total = add_slots(cpz, n3)
@@ -394,7 +394,11 @@
                 e_moves.append((e1.at[mine], e1.at[mine], {"a2": lax.rem(me2 + d2, n2), "a1": lax.rem(me1 + d1, n1)}))
     arrive([net.exchange(e_moves, e1.at[pl.ds(0, n1 * n2 - 1)])])
     e3[me3] = add_slots(e1, n1 * n2)
-    arrive(share(lambda p: e3.at[me3], e3, me3, peers3, on3))
+    e_last = share(lambda p: e3.at[me3], e3, me3, peers3, on3)
+    arrive([p3_half])
+    p3_moves = [(p3_out.at[p, core], p3_out.at[p, core], other) for p in peers3]
+    p3_copies = [net.exchange(p3_moves, p3_out.at[pl.ds(0, n3 - 1), 0])]
+    arrive(e_last)
     store(e3, e_out)
     arrive(p2_copies + p3_copies)
     net.finish()
@@ -442,7 +446,7 @@
         ar, bq, wx, zq = rank1 // n1, 128 // n2, wl // 2 // nx, n3 // n2
         hops = n3 - 1
         frames, parts = n1 * fl, hl // 2 // n3 // 8
-        outs = [(rank1, frames), (hl, 128), (n2, 8, 128), (wl, 128), (n3, 8, 128), (cz, 256), (n3, 8, 128)]
+        outs = [(rank1, frames), (hl, 128), (n2, 8, 128), (n3, 8, 128), (cz, 256), (n3, 8, 128)]
         scratch = [
             (tensor.shape, BF16), ((rank1, frames), F32), (u_height.shape, F32), (u_width.shape, F32), ((wl, 128), F32), *[(shape, F32) for shape in outs],
             ((256, 256), BF16), ((frames, 128), BF16), ((n3, fl, cz, hl), F32), ((2, hops, half, cz // 2, hl), F32), ((2, hops, fl - half, cz // 2, hl), F32),
@@ -460,7 +464,8 @@
             ((n3, cz, 256), F32), ((n3, cz, 256), F32), ((n2 * n1, 8, 128), F32),
         ]
         raws = list(outs)
-        raws[1], raws[3] = (n2, hl, 128), (n3, wl, 128)
+        raws[1] = (n2, hl, 128)
+        raws.insert(3, (n3, 2, wl // 2, 128))
         raw = pl.pallas_call(
             functools.partial(sweep_kernel, n1, n2, n3),
             out_shape=[jax.ShapeDtypeStruct(shape, F32) for shape in raws],

time: 200 us -> 197 us (0.985)
  Pallas kernels: 199 us -> 196 us
    pallas_call x1, Pallas kernels: 197 us -> 194 us  [local_sweep(): pl.pallas_call(functools.partial(sweep_kernel, n1, n2, n3), out_shape=[ja...]
where the time goes in v3:
time: 197 us; the launch traced here: 196 us
  Pallas kernels  196 us (99%)
    pallas_call x1, Pallas kernels, local_sweep(): pl.pallas_call(functools.partial(sweep_kernel, n1, n2, n3), out_shape=[ja...  194 us

profile of v3, /device:TPU:1, one launch (start us, length us, event | category | flops | bytes accessed | tf_op | source)
XLA Modules:
  0.0 196.5 jit_solution(1503672367965704247)
XLA Ops:
  0.6 193.6 %sweep.1 = (f32[48,384]{1,0:T(8,128)}, f32[4,256,128]{2,1,0:T(8,128)}, f32[4,8,128]{2,1,0:T(8,128)}, f32[8,2,64,128]{3,2,1,0:T(8,128)}, f32[8,8,128]{2,1,0:T(8,1...) custom-call(bf16[48,256,128]{2,1,0:T(8,128)(2,1)} %x_hbm.1, f32[48,384]{1,0:T(8,128)} %bitcast.4, f32[1024,128]{1,0:T(8,128)} %u2_hbm.1, ...), custom_call_target="tpu_custom_call" | custom-call | tf_op jit(solution)/shard_map/sweep/pallas_call | solution.py:469
  194.3 2.2 %finish.1 = (f32[48,384]{1,0:T(8,128)}, f32[1024,128]{1,0:T(8,128)}, f32[1024,128]{1,0:T(8,128)}, f32[6,16,32]{2,1,0:T(8,128)}, f32[1,1]{1,0:T(1,128)}) custom-call(f32[48,384]{1,0:T(8,128)} %get-tuple-element.17.refs_0_, f32[4,256,128]{2,1,0:T(8,128)} %get-tuple-element.18.refs_1_, f32[4,8,128]{2,1,0:T(8,128)} %get-tuple-element.19.refs_2_, ...), custom_call_target="tpu_custom_call" | custom-call | tf_op jit(solution)/shard_map/finish/pallas_call | solution.py:480

commit v4 on v3

--- a/solution.py
+++ b/solution.py
@@ -10,7 +10,7 @@
 F32 = jnp.float32
 BF16 = jnp.bfloat16
 MESH = pl.DeviceIdType.MESH
-EXCHANGES = 83
+EXCHANGES = 91
 NN = ((1,), (0,))
 NT = ((1,), (1,))
 TN = ((0,), (0,))
@@ -323,24 +323,34 @@
     bq = 128 // n2
     for a in range(ar):
         y3p[:, a] = dot(u2t, zf[a]).reshape(n2, bq, wl)
-    copies = share(lambda p: y3p.at[p], y3y, me2, peers2, on2)
+    y3y[me2] = y3p[me2]
+    ah = ar // 2
+    y3_copies = []
+    for a in (0, ah):
+        now = pl.ds(a, ah)
+        moves = [(y3p.at[p, now], y3y.at[me2, now], on2(p)) for p in peers2]
+        y3_copies.append(net.exchange(moves, y3y.at[pl.ds(0, n2 - 1), now]))
     p2_copies = share(lambda p: p2, p2_out, me2, peers2, on2)
-    y3y[me2] = y3p[me2]
-    arrive(copies)
-    y3o[...] = add_slots(y3y, n2).astype(BF16).reshape(ar * bq, wl)
 
     wx = wl // 2 // nx
     order = [d for k in range(1, reach) for d in (k, n3 - k)] + [reach]
     peer_of = {d: lax.rem(me3 + d, n3) for d in order}
-    y3z[me3] = y3o[...]
-    incoming = {n3 - d: net.send(y3o, y3z.at[me3], on3(peer_of[d])) for d in order}
+    incoming = {d: [] for d in order}
+    for k, a in enumerate((0, ah)):
+        arrive([y3_copies[k]])
+        rows = pl.ds(a * bq, ah * bq)
+        block = add_slots([y3y[q, a : a + ah] for q in range(n2)], n2).astype(BF16).reshape(ah * bq, wl)
+        y3o[rows, :] = block
+        y3z[me3, rows, :] = block
+        for d in order:
+            incoming[n3 - d].append(net.send(y3o.at[rows], y3z.at[me3, rows], on3(peer_of[d])))
     groups = [[0, 1, n3 - 1], [2, n3 - 2], [3, n3 - 3, 4]]
     pieces_x = []
     for group in groups:
         swaps = []
         for d in group:
             if d:
-                arrive([incoming[d]])
+                arrive(incoming[d])
             q = peer_of[d] if d else me3
             gp3[:, q] = dot(y3o[...], y3z[q], TN).reshape(2, wl // 2, wl)
             swaps.append((q, net.send(gp3.at[1 - core, q], c0.at[q], other)))

time: 197 us -> 195 us (0.990)
  Pallas kernels: 196 us -> 194 us
where the time goes in v4:
time: 195 us
  Pallas kernels  194 us (99%)
    pallas_call x1, Pallas kernels, local_sweep(): pl.pallas_call(functools.partial(sweep_kernel, n1, n2, n3), out_shape=[ja...  192 us

profile of v4, /device:TPU:1, one launch (start us, length us, event | category | flops | bytes accessed | tf_op | source)
XLA Modules:
  0.0 194.7 jit_solution(12273178001705631064)
XLA Ops:
  0.6 191.8 %sweep.1 = (f32[48,384]{1,0:T(8,128)}, f32[4,256,128]{2,1,0:T(8,128)}, f32[4,8,128]{2,1,0:T(8,128)}, f32[8,2,64,128]{3,2,1,0:T(8,128)}, f32[8,8,128]{2,1,0:T(8,1...) custom-call(bf16[48,256,128]{2,1,0:T(8,128)(2,1)} %x_hbm.1, f32[48,384]{1,0:T(8,128)} %bitcast.4, f32[1024,128]{1,0:T(8,128)} %u2_hbm.1, ...), custom_call_target="tpu_custom_call" | custom-call | tf_op jit(solution)/shard_map/sweep/pallas_call | solution.py:479
  192.5 2.2 %finish.1 = (f32[48,384]{1,0:T(8,128)}, f32[1024,128]{1,0:T(8,128)}, f32[1024,128]{1,0:T(8,128)}, f32[6,16,32]{2,1,0:T(8,128)}, f32[1,1]{1,0:T(1,128)}) custom-call(f32[48,384]{1,0:T(8,128)} %get-tuple-element.17.refs_0_, f32[4,256,128]{2,1,0:T(8,128)} %get-tuple-element.18.refs_1_, f32[4,8,128]{2,1,0:T(8,128)} %get-tuple-element.19.refs_2_, ...), custom_call_target="tpu_custom_call" | custom-call | tf_op jit(solution)/shard_map/finish/pallas_call | solution.py:490
